TPU v7x, 128 devices: a whole 4x4x4 slice. The times are simulated.
128 devices in a mesh: part: 1, data: 64 (over z, y, x), model: 2 (over core).
Axes of the slice: x: 4, y: 4, z: 4, core: 2. Of those that a mesh axis runs over, the one named last changes fastest.
Arguments:
- x: bfloat16 [2, 64, 1024, 1024], P(None, ('part', 'data'), 'model')
- lengths: int32 [2, 64], P(None, ('part', 'data'))
- norm_gain: bfloat16 [2, 1024], P(None, 'data')
- w_in: bfloat16 [2, 1024, 9216], P(None, 'data', 'model')
- w_kv: bfloat16 [2, 1024, 128], P(None, 'data')
- w_out: bfloat16 [2, 5120, 1024], P(None, 'model', 'data')
Outputs:
- output: bfloat16 [2, 64, 1024, 1024], P(None, ('part', 'data'), 'model')
All inputs are finite; a program needn't handle non-finite values.
Results may differ from a plain program's by a relative error of at most 0.0146278.
Values are sent between devices in bfloat16 or wider.
A program may use at most 1 GiB of HBM per device.

v0:
```python
import math
import jax
import jax.numpy as jnp
from jax import lax
from jax.sharding import PartitionSpec as P, NamedSharding

NORM_EPS = 1e-6
NEG_BIG = -1e30


def layer_norm(x_act, gain_vec):
    x_f32 = x_act.astype(jnp.float32)
    centered = x_f32 - jnp.mean(x_f32, axis=-1, keepdims=True)
    variance = jnp.mean(centered * centered, axis=-1, keepdims=True)
    return (centered * lax.rsqrt(variance + NORM_EPS) * gain_vec.astype(jnp.float32)).astype(jnp.bfloat16)


def attention(q_heads, k_all, v_all, seq_lens, q_offset):
    q_len = q_heads.shape[1]
    k_len = k_all.shape[1]
    head_dim = k_all.shape[2]
    scores = jnp.einsum("bqhc,bkc->bhqk", q_heads, k_all, preferred_element_type=jnp.float32) * (1.0 / math.sqrt(head_dim))
    q_pos = q_offset + lax.broadcasted_iota(jnp.int32, (q_len, 1), 0)
    k_pos = lax.broadcasted_iota(jnp.int32, (1, k_len), 1)
    allowed = (k_pos <= q_pos)[None, None] & (k_pos[None, None] < seq_lens[:, None, None, None])
    scores = jnp.where(allowed, scores, NEG_BIG)
    attn_probs = jax.nn.softmax(scores, axis=-1).astype(jnp.bfloat16)
    return jnp.einsum("bhqk,bkc->bqhc", attn_probs, v_all, preferred_element_type=jnp.float32).astype(jnp.bfloat16)


def layer_block(x_loc, seq_lens, gain_full, w_in3, w_kv_full, w_out3, n_model):
    n_seqs, t_loc, d_model = x_loc.shape
    head_dim = w_kv_full.shape[1] // 2
    ff_head = (w_in3.shape[2] - head_dim) // 2
    h_loc = layer_norm(x_loc, gain_full)
    h_all = lax.all_gather(h_loc, "model", axis=1, tiled=True)
    projected = jnp.einsum("btd,dhc->bthc", h_all, w_in3, preferred_element_type=jnp.float32).astype(jnp.bfloat16)
    kv_act = jnp.einsum("btd,dc->btc", h_all, w_kv_full, preferred_element_type=jnp.float32).astype(jnp.bfloat16)
    attn_out = attention(projected[..., :head_dim], kv_act[..., :head_dim], kv_act[..., head_dim:], seq_lens, 0)
    gate_act = projected[..., head_dim:head_dim + ff_head]
    up_act = projected[..., head_dim + ff_head:]
    mlp_out = (jax.nn.silu(gate_act.astype(jnp.float32)) * up_act.astype(jnp.float32)).astype(jnp.bfloat16)
    joined = jnp.concatenate([attn_out, mlp_out], axis=-1)
    group_sum = jnp.einsum("bthc,hcd->btd", joined, w_out3, preferred_element_type=jnp.float32).astype(jnp.bfloat16)
    received = lax.all_to_all(group_sum.reshape(n_seqs, n_model, t_loc, d_model), "model", 1, 1, tiled=True)
    z_sum = jnp.sum(received.astype(jnp.float32), axis=1)
    return (x_loc.astype(jnp.float32) + z_sum).astype(jnp.bfloat16)


def solution(mesh):
    n_model = mesh.shape["model"]
    act_spec = P(None, ("part", "data"), "model", None)

    def local_fn(x_blk, len_blk, gain_blk, w_in_blk, w_kv_blk, w_out_blk):
        head_dim = w_kv_blk.shape[2] // 2
        hidden = [x_blk[micro_idx] for micro_idx in range(x_blk.shape[0])]
        for layer_idx in range(gain_blk.shape[0]):
            gain_full = lax.all_gather(gain_blk[layer_idx], "data", axis=0, tiled=True)
            w_in_loc = lax.all_gather(w_in_blk[layer_idx], "data", axis=0, tiled=True)
            w_kv_full = lax.all_gather(w_kv_blk[layer_idx], "data", axis=0, tiled=True)
            w_out_loc = lax.all_gather(w_out_blk[layer_idx], "data", axis=1, tiled=True)
            d_model, in_loc = w_in_loc.shape
            out_loc = w_out_loc.shape[0]
            ff_loc = in_loc - out_loc
            heads_loc = (out_loc - ff_loc) // head_dim
            w_in3 = w_in_loc.reshape(d_model, heads_loc, in_loc // heads_loc)
            w_out3 = w_out_loc.reshape(heads_loc, out_loc // heads_loc, d_model)
            for micro_idx in range(len(hidden)):
                hidden[micro_idx] = layer_block(hidden[micro_idx], len_blk[micro_idx], gain_full, w_in3, w_kv_full, w_out3, n_model)
        return jnp.stack(hidden)

    return jax.shard_map(
        local_fn,
        mesh=mesh,
        in_specs=(act_spec, P(None, ("part", "data")), P(None, "data"), P(None, "data", "model"), P(None, "data", None), P(None, "model", "data")),
        out_specs=act_spec,
        check_vma=False,
    )
```

profile of v0, /device:TPU:1, one launch (start us, length us, event | category | flops | bytes accessed | tf_op | source)
XLA Modules:
  0.0 922.3 jit_solution(18362114738596128818)
XLA Ops:
  6.5 2.0 convert_reduce_fusion.5
  8.6 2.2 fusion.58
  10.9 0.7 slice_bitcast_fusion.25
  11.6 1.2 dynamic-slice
  14.0 153.6 %all-reduce.2 = (bf16[1024]{0:T(1024)(128)(2,1)S(1)}, bf16[1024]{0:T(1024)(128)(2,1)S(1)}) all-reduce(bf16[1024]{0:T(1024)(128)(2,1)S(1)} %dynamic-update-slice.1, bf16[1024]{0:T(1024)(128)(2,1)S(1)} %dynamic-update-slice), channel_id=6, replica_groups=mesh['part'=1,'data'=64,'model'=2] {'data'}, use_global_device_ids=true, to_apply=%add.1 | all-reduce | flops 2048 | bytes 8192
  167.6 2.0 fusion.63
  169.6 0.7 all-gather.17.cloned.1.call-update
  170.4 0.7 fusion.155
  171.2 0.7 fusion.154
  172.0 0.5 all-gather.31.cloned.1.call-update
  172.5 0.5 all-gather.29.cloned.1.call-update
  173.1 0.6 fusion.156
  173.7 143.5 %all-gather.1 = bf16[1,1024,128]{2,1,0:T(8,128)(2,1)S(1)} all-gather(bf16[1,16,128]{2,1,0:T(8,128)(2,1)S(1)} %get-tuple-element.26), channel_id=3, replica_groups=mesh['part'=1,'data'=64,'model'=2] {'data'}, dimensions={1}, use_global_device_ids=true | all-gather | bytes 266240 | tf_op jit(solution)/shard_map/all_gather | solution.py:60
  317.2 0.7 fusion.157
  317.9 0.7 iota_compare_fusion.1
  318.9 0.6 iota_compare_fusion.2
  319.9 0.6 convert_element_type.489
  320.5 2.4 fusion.125
  322.9 2.4 fusion.131
  325.4 8.1 copy.17
  333.5 43.0 %all-gather.25.cloned.1.call-done = bf16[1,1024,4608]{2,1,0:T(8,128)(2,1)} async-done(((bf16[1,16,4608]{2,1,0:T(8,128)(2,1)}), bf16[1,1024,4608]{2,1,0:T(8,128)(2,1)}) %all-gather.25.cloned.1.call-update) | async-done | bytes 9437200 | tf_op jit(solution)/shard_map/all_gather | solution.py:59
  376.5 12.7 %copy.15 = bf16[1,1024,4608]{1,2,0:T(8,128)(2,1)} copy(bf16[1,1024,4608]{2,1,0:T(8,128)(2,1)} %all-gather.25.cloned.1.call-done) | data formatting | bytes 18874368 | tf_op jit(solution)/shard_map/all_gather | solution.py:59
  389.1 13.3 %convert_bitcast_fusion.1 = bf16[1,1024,8,576]{1,3,2,0:T(8,128)(2,1)S(1)} fusion(bf16[1024,8,576]{0,2,1:T(8,128)(2,1)} %bitcast.387, bf16[1,1024,1024]{2,1,0:T(8,128)(2,1)} %all-gather.21.cloned.1.call-done), kind=kOutput, calls=%fused_computation.37 | convolution fusion | flops 9668395008 | bytes 20971520 | tf_op jit(solution)/shard_map/btd,dhc->bthc/dot_general | solution.py:37
  402.4 2.7 fusion.33
  405.1 13.5 %fusion.6 = (f32[8,1024]{1,0:T(8,128)S(1)}, f32[1024,1024,8]{1,0,2:T(8,128)}) fusion(pred[1024,1024]{0,1:T(8,128)(4,1)S(1)} %fusion.48, bf16[1,1024,8,576]{1,3,2,0:T(8,128)(2,1)S(1)} %convert_bitcast_fusion.1, bf16[1,1024,128]{1,2,0:T(8,128)(2,1)S(1)} %fusion.125), kind=kOutput, calls=%fused_computation.18 | convolution fusion | flops 1098899456 | bytes 35815424 | tf_op jit(solution)/shard_map/bqhc,bkc->bhqk/dot_general | solution.py:22
  418.6 14.2 %fusion.2 = f32[8,1024]{1,0:T(8,128)S(1)} fusion(f32[1024,1024,8]{1,0,2:T(8,128)} %get-tuple-element.34, f32[8,1024]{1,0:T(8,128)S(1)} %get-tuple-element.33, pred[1024,1024]{0,1:T(8,128)(4,1)S(1)} %fusion.48), kind=kLoop, calls=%fused_computation.14 | loop fusion | flops 33546240 | bytes 34668544 | tf_op jit(solution)/shard_map/reduce_sum | solution.py:27
  432.8 15.8 %fusion.101 = bf16[1,1024,8,64]{1,3,2,0:T(8,128)(2,1)} fusion(f32[8,1024]{1,0:T(8,128)S(1)} %fusion.2, f32[8,1024]{1,0:T(8,128)S(1)} %get-tuple-element.33, f32[1024,1024,8]{1,0,2:T(8,128)} %get-tuple-element.34, pred[1024,1024]{0,1:T(8,128)(4,1)S(1)} %fusion.48, bf16[1,1024,128]{1,2,0:T(8,128)(2,1)S(1)} %fusion.125), kind=kOutput, calls=%fused_computation.147 | convolution fusion | flops 1116209152 | bytes 35848192 | tf_op jit(solution)/shard_map/bhqk,bkc->bqhc/dot_general | solution.py:28
  448.5 9.5 %bitcast_convert_fusion.1 = bf16[1024,1024]{1,0:T(8,128)(2,1)} fusion(bf16[8,320,1024]{2,1,0:T(8,128)(2,1)} %bitcast.393, bf16[1,1024,8,256]{1,3,2,0:T(8,128)(2,1)S(1)} %fusion.33, bf16[1,1024,8,64]{1,3,2,0:T(8,128)(2,1)} %fusion.101), kind=kOutput, calls=%fused_computation.77 | convolution fusion | flops 5380243456 | bytes 12582912 | tf_op jit(solution)/shard_map/bthc,hcd->btd/dot_general | solution.py:44
  458.0 18.1 %all-to-all-start.2 = ((bf16[1,2,512,1024]{3,2,0,1:T(8,128)(2,1)}), bf16[1,2,512,1024]{3,2,0,1:T(8,128)(2,1)}, u32[]{:S(2)}, u32[]{:S(2)}) async-start(bf16[1,2,512,1024]{3,2,0,1:T(8,128)(2,1)} %bitcast.396), calls=%async_computation.2 | async-start | bytes 4194304 | tf_op jit(solution)/shard_map/all_to_all | solution.py:45
  476.1 13.3 %convert_bitcast_fusion.3 = bf16[1,1024,8,576]{1,3,2,0:T(8,128)(2,1)S(1)} fusion(bf16[1024,8,576]{0,2,1:T(8,128)(2,1)} %bitcast.388, bf16[1,1024,1024]{2,1,0:T(8,128)(2,1)} %all-gather.17.cloned.1.call-done), kind=kOutput, calls=%fused_computation.39 | convolution fusion | flops 9668395008 | bytes 20971520 | tf_op jit(solution)/shard_map/btd,dhc->bthc/dot_general | solution.py:37
  489.4 13.5 %fusion.4 = (f32[8,1024]{1,0:T(8,128)S(1)}, f32[1024,1024,8]{1,0,2:T(8,128)}) fusion(pred[1024,1024]{0,1:T(8,128)(4,1)S(1)} %fusion.49, bf16[1,1024,8,576]{1,3,2,0:T(8,128)(2,1)S(1)} %convert_bitcast_fusion.3, bf16[1,1024,128]{1,2,0:T(8,128)(2,1)S(1)} %fusion.131), kind=kOutput, calls=%fused_computation.16 | convolution fusion | flops 1098899456 | bytes 35815424 | tf_op jit(solution)/shard_map/bqhc,bkc->bhqk/dot_general | solution.py:22
  502.9 2.7 fusion.35
  505.5 14.2 %fusion = f32[8,1024]{1,0:T(8,128)S(1)} fusion(f32[1024,1024,8]{1,0,2:T(8,128)} %get-tuple-element.32, f32[8,1024]{1,0:T(8,128)S(1)} %get-tuple-element.31, pred[1024,1024]{0,1:T(8,128)(4,1)S(1)} %fusion.49), kind=kLoop, calls=%fused_computation.12 | loop fusion | flops 33546240 | bytes 34668544 | tf_op jit(solution)/shard_map/reduce_sum | solution.py:27
  519.7 16.0 %fusion.107 = bf16[1,1024,8,64]{1,3,2,0:T(8,128)(2,1)} fusion(f32[8,1024]{1,0:T(8,128)S(1)} %fusion, f32[8,1024]{1,0:T(8,128)S(1)} %get-tuple-element.31, f32[1024,1024,8]{1,0,2:T(8,128)} %get-tuple-element.32, pred[1024,1024]{0,1:T(8,128)(4,1)S(1)} %fusion.49, bf16[1,1024,128]{1,2,0:T(8,128)(2,1)S(1)} %fusion.131), kind=kOutput, calls=%fused_computation.149 | convolution fusion | flops 1116209152 | bytes 35848192 | tf_op jit(solution)/shard_map/bhqk,bkc->bqhc/dot_general | solution.py:28
  535.7 9.5 %bitcast_convert_fusion.3 = bf16[1024,1024]{1,0:T(8,128)(2,1)} fusion(bf16[8,320,1024]{2,1,0:T(8,128)(2,1)} %bitcast.394, bf16[1,1024,8,256]{1,3,2,0:T(8,128)(2,1)S(1)} %fusion.35, bf16[1,1024,8,64]{1,3,2,0:T(8,128)(2,1)} %fusion.107), kind=kOutput, calls=%fused_computation.79 | convolution fusion | flops 5380243456 | bytes 12582912 | tf_op jit(solution)/shard_map/bthc,hcd->btd/dot_general | solution.py:44
  545.2 4.9 all-to-all-start
  550.0 3.7 convert_reduce_fusion.1
  553.8 2.4 convert_reduce_fusion.3
  556.2 0.6 convert_reduce_fusion.7
  556.8 0.9 multiply_reduce_fusion.1
  557.8 2.1 multiply_convert_fusion.1
  559.9 144.4 %all-gather.5 = bf16[1,1024,128]{2,1,0:T(8,128)(2,1)S(1)} all-gather(bf16[1,16,128]{2,1,0:T(8,128)(2,1)S(1)} %copy-done.15), channel_id=7, replica_groups=mesh['part'=1,'data'=64,'model'=2] {'data'}, dimensions={1}, use_global_device_ids=true | all-gather | bytes 266240 | tf_op jit(solution)/shard_map/all_gather | solution.py:60
  704.3 8.1 copy.21
  712.5 12.7 %copy.19 = bf16[1,1024,4608]{1,2,0:T(8,128)(2,1)} copy(bf16[1,1024,4608]{2,1,0:T(8,128)(2,1)} %all-gather.29.cloned.1.call-done) | data formatting | bytes 18874368 | tf_op jit(solution)/shard_map/all_gather | solution.py:59
  725.1 13.3 %convert_bitcast_fusion = bf16[1,1024,8,576]{1,3,2,0:T(8,128)(2,1)S(1)} fusion(bf16[1024,8,576]{0,2,1:T(8,128)(2,1)} %bitcast.385, bf16[1,1024,1024]{2,1,0:T(8,128)(2,1)} %all-gather.23.cloned.1.call-done), kind=kOutput, calls=%fused_computation.36 | convolution fusion | flops 9668395008 | bytes 20971520 | tf_op jit(solution)/shard_map/btd,dhc->bthc/dot_general | solution.py:37
  738.4 4.0 fusion.32
  742.4 0.8 fusion.122
  743.3 13.5 %fusion.7 = (f32[8,1024]{1,0:T(8,128)S(1)}, f32[1024,1024,8]{1,0,2:T(8,128)}) fusion(pred[1024,1024]{0,1:T(8,128)(4,1)S(1)} %fusion.48, bf16[1,1024,8,576]{1,3,2,0:T(8,128)(2,1)S(1)} %convert_bitcast_fusion, bf16[1,1024,128]{1,2,0:T(8,128)(2,1)S(1)} %fusion.122), kind=kOutput, calls=%fused_computation.19 | convolution fusion | flops 1098899456 | bytes 35815424 | tf_op jit(solution)/shard_map/bqhc,bkc->bhqk/dot_general | solution.py:22
  756.7 14.4 %fusion.3 = f32[8,1024]{1,0:T(8,128)S(1)} fusion(f32[1024,1024,8]{1,0,2:T(8,128)} %get-tuple-element.38, f32[8,1024]{1,0:T(8,128)S(1)} %get-tuple-element.37, pred[1024,1024]{0,1:T(8,128)(4,1)S(1)} %fusion.48), kind=kLoop, calls=%fused_computation.15 | loop fusion | flops 33546240 | bytes 34668544 | tf_op jit(solution)/shard_map/reduce_sum | solution.py:27
  771.2 14.9 %fusion.98 = bf16[1,1024,8,64]{1,3,2,0:T(8,128)(2,1)S(1)} fusion(f32[8,1024]{1,0:T(8,128)S(1)} %fusion.3, f32[8,1024]{1,0:T(8,128)S(1)} %get-tuple-element.37, f32[1024,1024,8]{1,0,2:T(8,128)} %get-tuple-element.38, pred[1024,1024]{0,1:T(8,128)(4,1)S(1)} %fusion.48, bf16[1,1024,128]{1,2,0:T(8,128)(2,1)S(1)} %fusion.122), kind=kOutput, calls=%fused_computation.146 | convolution fusion | flops 1116209152 | bytes 35848192 | tf_op jit(solution)/shard_map/bhqk,bkc->bqhc/dot_general | solution.py:28
  786.2 9.1 bitcast_convert_fusion
  795.3 31.9 %all-to-all-start.3 = ((bf16[1,2,512,1024]{3,2,0,1:T(8,128)(2,1)}), bf16[1,2,512,1024]{3,2,0,1:T(8,128)(2,1)S(1)}, u32[]{:S(2)}, u32[]{:S(2)}) async-start(bf16[1,2,512,1024]{3,2,0,1:T(8,128)(2,1)} %bitcast.395), calls=%async_computation.3 | async-start | bytes 4194304 | tf_op jit(solution)/shard_map/all_to_all | solution.py:45
  827.2 13.3 %convert_bitcast_fusion.2 = bf16[1,1024,8,576]{1,3,2,0:T(8,128)(2,1)S(1)} fusion(bf16[1024,8,576]{0,2,1:T(8,128)(2,1)} %bitcast.386, bf16[1,1024,1024]{2,1,0:T(8,128)(2,1)} %all-gather.19.cloned.1.call-done), kind=kOutput, calls=%fused_computation.38 | convolution fusion | flops 9668395008 | bytes 20971520 | tf_op jit(solution)/shard_map/btd,dhc->bthc/dot_general | solution.py:37
  840.5 4.1 fusion.34
  844.6 0.8 fusion.128
  845.5 13.5 %fusion.5 = (f32[8,1024]{1,0:T(8,128)S(1)}, f32[1024,1024,8]{1,0,2:T(8,128)}) fusion(pred[1024,1024]{0,1:T(8,128)(4,1)S(1)} %copy-done.8, bf16[1,1024,8,576]{1,3,2,0:T(8,128)(2,1)S(1)} %convert_bitcast_fusion.2, bf16[1,1024,128]{1,2,0:T(8,128)(2,1)S(1)} %fusion.128), kind=kOutput, calls=%fused_computation.17 | convolution fusion | flops 1098899456 | bytes 35815424 | tf_op jit(solution)/shard_map/bqhc,bkc->bhqk/dot_general | solution.py:22
  858.9 14.2 %fusion.1 = f32[8,1024]{1,0:T(8,128)S(1)} fusion(f32[1024,1024,8]{1,0,2:T(8,128)} %get-tuple-element.36, f32[8,1024]{1,0:T(8,128)S(1)} %get-tuple-element.35, pred[1024,1024]{0,1:T(8,128)(4,1)S(1)} %copy-done.8), kind=kLoop, calls=%fused_computation.13 | loop fusion | flops 33546240 | bytes 34668544 | tf_op jit(solution)/shard_map/reduce_sum | solution.py:27
  873.1 14.9 %fusion.104 = bf16[1,1024,8,64]{1,3,2,0:T(8,128)(2,1)S(1)} fusion(f32[8,1024]{1,0:T(8,128)S(1)} %fusion.1, f32[8,1024]{1,0:T(8,128)S(1)} %get-tuple-element.35, f32[1024,1024,8]{1,0,2:T(8,128)} %get-tuple-element.36, pred[1024,1024]{0,1:T(8,128)(4,1)S(1)} %copy-done.8, bf16[1,1024,128]{1,2,0:T(8,128)(2,1)S(1)} %fusion.128), kind=kOutput, calls=%fused_computation.148 | convolution fusion | flops 1116209152 | bytes 35848192 | tf_op jit(solution)/shard_map/bhqk,bkc->bqhc/dot_general | solution.py:28
  888.0 10.0 %bitcast_convert_fusion.2 = bf16[1024,1024]{1,0:T(8,128)(2,1)} fusion(bf16[8,320,1024]{2,1,0:T(8,128)(2,1)} %bitcast.389, bf16[1,1024,8,256]{1,3,2,0:T(8,128)(2,1)} %fusion.34, bf16[1,1024,8,64]{1,3,2,0:T(8,128)(2,1)S(1)} %fusion.104), kind=kOutput, calls=%fused_computation.78 | convolution fusion | flops 5380243456 | bytes 12582912 | tf_op jit(solution)/shard_map/bthc,hcd->btd/dot_general | solution.py:44
  898.0 1.4 copy-done.9
  899.4 4.8 all-to-all-start.1
  904.2 3.7 convert_reduce_fusion
  907.9 2.5 convert_reduce_fusion.2
  910.8 4.2 fusion.79
  (79 shorter events, 2.0 us)
Async XLA Ops:
  6.5 161.0 %copy-start = (bf16[2,1,512,1024]{3,2,1,0:T(8,128)(2,1)S(1)}, bf16[2,1,512,1024]{3,2,1,0:T(8,128)(2,1)}, u32[]{:S(2)}) copy-start(bf16[2,1,512,1024]{3,2,1,0:T(8,128)(2,1)} %param.6) | copy-start | bytes 6291460
  6.5 314.0 %all-gather.21.cloned.1.call-start = ((), (), s32[]{:S(2)}) async-start(), calls=%async_computation.6 | async-start | bytes 3145728 | tf_op jit(solution)/shard_map/all_gather | solution.py:36
  6.5 163.8 %copy-start.13 = (bf16[2,2560,16]{1,2,0:T(8,128)(2,1)S(1)}, bf16[2,2560,16]{1,2,0:T(8,128)(2,1)}, u32[]{:S(2)}) copy-start(bf16[2,2560,16]{1,2,0:T(8,128)(2,1)} %param.11) | copy-start | bytes 491524
  6.5 164.6 %copy-start.12 = (bf16[2,16,4608]{2,1,0:T(8,128)(2,1)S(1)}, bf16[2,16,4608]{2,1,0:T(8,128)(2,1)}, u32[]{:S(2)}) copy-start(bf16[2,16,4608]{2,1,0:T(8,128)(2,1)} %param.9) | copy-start | bytes 884740
  8.6 164.5 %copy-start.16 = (bf16[2,16,128]{2,1,0:T(8,128)(2,1)S(1)}, bf16[2,16,128]{2,1,0:T(8,128)(2,1)}, u32[]{:S(2)}) copy-start(bf16[2,16,128]{2,1,0:T(8,128)(2,1)} %param.10) | copy-start | bytes 24580
  8.6 308.6 %copy-start.17 = (s32[2,1]{0,1:T(1,128)S(1)}, s32[2,1]{0,1:T(1,128)}, u32[]{:S(2)}) copy-start(s32[2,1]{0,1:T(1,128)} %param.7) | copy-start | bytes 28
  169.6 153.3 %all-gather.17.cloned.1.call-start = ((), (), s32[]{:S(2)}) async-start(), calls=%async_computation.4 | async-start | bytes 3145728 | tf_op jit(solution)/shard_map/all_gather | solution.py:36
  170.3 155.0 %all-gather.27.cloned.1.call-start = ((), (), s32[]{:S(2)}) async-start(), calls=%async_computation.9 | async-start | bytes 5324800 | tf_op jit(solution)/shard_map/all_gather | solution.py:61
  171.1 205.3 %all-gather.25.cloned.1.call-start = ((), (), s32[]{:S(2)}) async-start(), calls=%async_computation.8 | async-start | bytes 9584640 | tf_op jit(solution)/shard_map/all_gather | solution.py:59
  171.9 532.4 %all-gather.31.cloned.1.call-start = ((), (), s32[]{:S(2)}) async-start(), calls=%async_computation.11 | async-start | bytes 5324800 | tf_op jit(solution)/shard_map/all_gather | solution.py:61
  172.5 539.9 %all-gather.29.cloned.1.call-start = ((), (), s32[]{:S(2)}) async-start(), calls=%async_computation.10 | async-start | bytes 9584640 | tf_op jit(solution)/shard_map/all_gather | solution.py:59
  319.9 199.9 %copy-start.7 = (pred[1024,1024]{0,1:T(8,128)(4,1)}, pred[1024,1024]{0,1:T(8,128)(4,1)S(1)}, u32[]{:S(2)}) copy-start(pred[1024,1024]{0,1:T(8,128)(4,1)S(1)} %fusion.49) | copy-start | bytes 3145732
  458.0 87.1 %all-to-all-start.2 = ((bf16[1,2,512,1024]{3,2,0,1:T(8,128)(2,1)}), bf16[1,2,512,1024]{3,2,0,1:T(8,128)(2,1)}, u32[]{:S(2)}, u32[]{:S(2)}) async-start(bf16[1,2,512,1024]{3,2,0,1:T(8,128)(2,1)} %bitcast.396), calls=%async_computation.2 | async-start | bytes 4194304 | tf_op jit(solution)/shard_map/all_to_all | solution.py:45
  545.2 8.6 all-to-all-start
  550.0 6.2 copy-start.1
  550.0 175.1 %all-gather.23.cloned.1.call-start = ((), (), s32[]{:S(2)}) async-start(), calls=%async_computation.7 | async-start | bytes 3145728 | tf_op jit(solution)/shard_map/all_gather | solution.py:36
  553.8 2.5 copy-start.3
  556.2 1.5 copy-start.5
  556.2 1.5 copy-start.14
  557.7 2.2 copy-start.15
  559.8 267.4 %all-gather.19.cloned.1.call-start = ((), (), s32[]{:S(2)}) async-start(), calls=%async_computation.5 | async-start | bytes 3145728 | tf_op jit(solution)/shard_map/all_gather | solution.py:36
  738.4 4.0 copy-start.11
  756.7 29.4 %slice-start = ((s8[5242880]{0:T(1024)(128)(4,1)}), s8[4194304]{0:T(1024)(128)(4,1)S(1)}, s32[]{:S(2)}) async-start(s8[5242880]{0:T(1024)(128)(4,1)} %bitcast.390), calls=%async_computation.12 | async-start | bytes 8388608
  771.2 15.0 %slice-start.1 = ((s8[5242880]{0:T(1024)(128)(4,1)}), s8[1048576]{0:T(1024)(128)(4,1)S(1)}, s32[]{:S(2)}) async-start(s8[5242880]{0:T(1024)(128)(4,1)} %bitcast.390), calls=%async_computation.13 | async-start | bytes 2097152
  795.3 102.7 %all-to-all-start.3 = ((bf16[1,2,512,1024]{3,2,0,1:T(8,128)(2,1)}), bf16[1,2,512,1024]{3,2,0,1:T(8,128)(2,1)S(1)}, u32[]{:S(2)}, u32[]{:S(2)}) async-start(bf16[1,2,512,1024]{3,2,0,1:T(8,128)(2,1)} %bitcast.395), calls=%async_computation.3 | async-start | bytes 4194304 | tf_op jit(solution)/shard_map/all_to_all | solution.py:45
  840.5 4.1 copy-start.10
  840.5 4.9 copy-start.8
  898.0 1.4 copy-start.9
  899.4 8.6 all-to-all-start.1
  904.2 6.2 copy-start.2
  907.9 2.5 copy-start.4
  907.9 2.9 copy-start.6
Sparse Core Ops, SparseCore 0:
  169.7 34.8 all-gather.20
  206.2 14.6 all-gather.16
  223.8 69.3 all-gather.26
  295.8 80.6 all-gather.24
  379.2 67.9 all-gather.30
  449.8 80.5 all-gather.28
  560.0 8.4 all-gather.22
  712.5 34.5 all-gather.18
where the time goes:
time: 934 us; the launch traced here: 922 us
  blocking collectives  442 us (47%)
  matrix products  213 us (23%)
  other arithmetic  99.5 us (11%)
  starting transfers between devices  60 us (6%)
  local copies, waits for them, and re-layouts  48.4 us (5%)
  waiting for transfers between devices  44.9 us (5%)
  between operations  15 us (2%)
    all_gather x2, blocking collectives, local_fn(): w_kv_full = lax.all_gather(w_kv_blk[layer_idx], 'data', axis=0, tiled=True)  288 us
    unnamed x1, blocking collectives  154 us
    dot_general x4, matrix products, attention(): jnp.einsum('bhqk,bkc->bqhc', attn_probs, v_all, preferred_element_type=jn...  61.6 us
    all_to_all x4, starting transfers between devices, layer_block(): lax.all_to_all(group_sum.reshape(n_seqs, n_model, t_loc, d_model), 'model...  59.7 us
    reduce_sum x4, other arithmetic, attention(): attn_probs = jax.nn.softmax(scores, axis=-1).astype(jnp.bfloat16)  57.1 us
    dot_general x4, matrix products, attention(): jnp.einsum('bqhc,bkc->bhqk', q_heads, k_all, preferred_element_type=jnp.f...  53.8 us
    dot_general x4, matrix products, layer_block(): jnp.einsum('btd,dhc->bthc', h_all, w_in3, preferred_element_type=jnp.floa...  53.1 us
    all_gather x2, waiting for transfers between devices, local_fn(): w_in_loc = lax.all_gather(w_in_blk[layer_idx], 'data', axis=0, tiled=True)  43 us
  transfers between devices with their start and end apart: 12, of which 1 were waited for; matrix products, arithmetic and copies ran while one was open for 37% of the time, Pallas kernels for 0%

commit v1 on v0

v1 whole, which is shorter than its diff:
```python
import functools
import math

import jax
import jax.numpy as jnp
from jax import lax
from jax.experimental import pallas as pl
from jax.experimental.pallas import tpu as pltpu
from jax.sharding import PartitionSpec as P

MESH = pl.DeviceIdType.MESH
NORM_EPS = 1e-6
MASKED = -3e38
SIDE = 4
ROTATIONS = (("x", "y", "z"), ("y", "z", "x"), ("z", "x", "y"))
TILE = 256
DO_COMM = True
DO_COMPUTE = True


def mesh_kernel(dims, x_hbm, lens_ref, small_hbm, big_hbm, y_hbm,
                wsmall, wbig, xbuf, hbuf, kbuf, vbuf, acc, joined, zsend, zrecv, gain_buf,
                own_sem, wsend, wrecv, io_sem, hsend, hrecv, zs_sem, zr_sem):
    n_micro, n_layers, n_chunks, t_loc, d_model, head_dim, ff_head = dims
    n_total = n_layers * n_chunks
    pair_q, pair_f = 2 * head_dim, 2 * ff_head
    in_cols = pair_q + 2 * pair_f
    seq = 2 * t_loc
    me = lax.axis_index("data")
    core = lax.axis_index("model")
    pos = {"x": lax.rem(me, SIDE), "y": lax.rem(me // SIDE, SIDE), "z": me // (SIDE * SIDE)}
    stride = {"x": 1, "y": SIDE, "z": SIDE * SIDE}

    def shifted(axis, step):
        moved = lax.rem(pos[axis] + SIDE + step, SIDE)
        return moved, me + (moved - pos[axis]) * stride[axis]

    near = {(a, s): shifted(a, s) for a in "xyz" for s in (1, -1)}
    sibling = {"model": 1 - core}

    barrier = pltpu.get_barrier_semaphore()
    for key in near:
        pl.semaphore_signal(barrier, inc=1, device_id={"data": near[key][1]}, device_id_type=MESH)
    pl.semaphore_signal(barrier, inc=1, device_id=sibling, device_id_type=MESH)
    pl.semaphore_wait(barrier, 7)

    big_parts = ((0, pair_q + pair_f), (pair_q + pair_f, in_cols), (in_cols, wbig.shape[-1]))
    small_parts = ((0, 256), (256, 384), (384, 512))

    class Chunk:
        def __init__(self, buf, src, parts, sem_idx):
            self.buf, self.src, self.parts, self.sem = buf, src, parts, sem_idx

        def region(self, where, cols):
            return self.buf.at[where["z"], where["y"], where["x"], :, pl.ds(cols[0], cols[1] - cols[0])]

        def own(self):
            return pltpu.make_async_copy(self.src, self.buf.at[pos["z"], pos["y"], pos["x"]], own_sem.at[self.sem])

        def send(self, k):
            phase, second = k // 2, k % 2
            for rot, (lo, hi) in zip(ROTATIONS, self.parts):
                axis = rot[phase]
                mid = lo + (((hi - lo) // 128 + 1) // 2) * 128
                for sign in (1, -1):
                    where = {a: slice(None) for a in rot[:phase]}
                    where.update({a: pos[a] for a in rot[phase:]})
                    cols = (lo, hi)
                    if second:
                        where[axis] = near[axis, -sign][0]
                        if phase == 0:
                            cols = (lo, mid) if sign == 1 else (mid, hi)
                            if cols[0] == cols[1]:
                                continue
                        else:
                            where[rot[0]] = pl.ds(0, 2) if sign == 1 else pl.ds(2, 2)
                    dst = self.region(where, cols)
                    src = self.src.at[:, pl.ds(cols[0], cols[1] - cols[0])] if k == 0 else dst
                    pltpu.make_async_remote_copy(
                        src_ref=src, dst_ref=dst, send_sem=wsend.at[self.sem, k], recv_sem=wrecv.at[self.sem, k],
                        device_id={"data": near[axis, sign][1]}, device_id_type=MESH).start()

        def bytes_of(self, k):
            ref = (self.buf.at[0, 0, pl.ds(0, 2)], self.buf.at[0, 0, 0], self.buf.at[0, pl.ds(0, 2)],
                   self.buf.at[0, 0], self.buf.at[pl.ds(0, 2)], self.buf.at[0])[k]
            return pltpu.make_async_remote_copy(
                src_ref=ref, dst_ref=ref, send_sem=wsend.at[self.sem, k], recv_sem=wrecv.at[self.sem, k],
                device_id={"data": near["x", 1][1]}, device_id_type=MESH)

        def step(self, k):
            if not DO_COMM:
                return
            if k == 0:
                self.own().start()
            else:
                self.bytes_of(k - 1).wait_recv()
            if k == 2:
                self.own().wait()
            if k < 6:
                self.send(k)

        def finish(self):
            if not DO_COMM:
                return
            for k in range(6):
                self.bytes_of(k).wait_send()

    small = Chunk(wsmall, small_hbm, small_parts, n_total)

    def big(n):
        return Chunk(wbig.at[n], big_hbm.at[n], big_parts, n)

    def step(n, k):
        if isinstance(n, int):
            if n < n_total:
                big(n).step(k)
        else:
            @pl.when(n < n_total)
            def _():
                big(n).step(k)

    def load_x(m):
        return pltpu.make_async_copy(x_hbm.at[m], xbuf.at[m], io_sem.at[m])

    def store_y(m):
        return pltpu.make_async_copy(xbuf.at[m], y_hbm.at[m], io_sem.at[m])

    def send_h(m):
        rows = hbuf.at[m, pl.ds(pl.multiple_of(core * t_loc, t_loc), t_loc)]
        return pltpu.make_async_remote_copy(src_ref=rows, dst_ref=rows, send_sem=hsend.at[m], recv_sem=hrecv.at[m],
                                            device_id=sibling, device_id_type=MESH)

    def send_z(m):
        return pltpu.make_async_remote_copy(src_ref=zsend.at[m], dst_ref=zrecv.at[m], send_sem=zs_sem.at[m],
                                            recv_sem=zr_sem.at[m], device_id=sibling, device_id_type=MESH)

    norm_rows = 32

    def norm(m, layer):
        gain = gain_buf[layer]

        def rows_of(r, carry):
            at = pl.multiple_of(r * norm_rows, norm_rows)
            x_f32 = xbuf[m, pl.ds(at, norm_rows), :].astype(jnp.float32)
            centered = x_f32 - jnp.mean(x_f32, axis=-1, keepdims=True)
            variance = jnp.mean(centered * centered, axis=-1, keepdims=True)
            h_act = (centered * lax.rsqrt(variance + NORM_EPS) * gain).astype(jnp.bfloat16)
            hbuf[m, pl.ds(pl.multiple_of(core * t_loc + at, norm_rows), norm_rows), :] = h_act
            return carry

        lax.fori_loop(0, t_loc // norm_rows, rows_of, 0)

    def keys_values(m, layer):
        w_kv = wsmall[:, :, :, :, pl.ds(pl.multiple_of(layer * 256, 128), 128)].reshape(d_model, 2 * head_dim)
        lane = lax.broadcasted_iota(jnp.int32, (TILE, 2 * head_dim), 1)
        low = lane < head_dim
        length = lens_ref[m]

        def rows_of(r, carry):
            at = pl.multiple_of(r * TILE, TILE)
            kv_f32 = jnp.dot(hbuf[m, pl.ds(at, TILE), :], w_kv, preferred_element_type=jnp.float32)
            kv_f32 = kv_f32.astype(jnp.bfloat16).astype(jnp.float32)
            vk_f32 = pltpu.roll(kv_f32, head_dim, 1)
            key_pos = at + lax.broadcasted_iota(jnp.int32, (TILE, 2 * head_dim), 0)
            bias = jnp.where(key_pos < length, 0.0, MASKED)
            k_low = jnp.where(low, kv_f32, jnp.where(lane == head_dim, bias, 0.0))
            k_high = jnp.where(low, jnp.where(lane == 0, bias, 0.0), vk_f32)
            kbuf[m, 0, pl.ds(at, TILE), :] = k_low.astype(jnp.bfloat16)
            kbuf[m, 1, pl.ds(at, TILE), :] = k_high.astype(jnp.bfloat16)
            vbuf[m, 0, pl.ds(at, TILE), :] = jnp.where(low, vk_f32, 0.0).astype(jnp.bfloat16)
            vbuf[m, 1, pl.ds(at, TILE), :] = jnp.where(low, 0.0, kv_f32).astype(jnp.bfloat16)
            return carry

        lax.fori_loop(0, seq // TILE, rows_of, 0)

    exp_scale = (1.0 / math.sqrt(head_dim)) * math.log2(math.e)

    def body(n, c, m):
        lane = lax.broadcasted_iota(jnp.int32, (TILE, pair_q), 1)
        tri = (lax.broadcasted_iota(jnp.int32, (TILE, TILE), 1) <= lax.broadcasted_iota(jnp.int32, (TILE, TILE), 0))
        for i in range(seq // TILE):
            rows = pl.ds(i * TILE, TILE)
            n_keys = (i + 1) * TILE
            h_rows = hbuf[m, rows, :]

            def weight(lo, hi):
                return wbig[n, :, :, :, :, lo:hi].reshape(d_model, hi - lo)

            q = jnp.dot(h_rows, weight(0, pair_q), preferred_element_type=jnp.float32).astype(jnp.bfloat16)
            one = jnp.ones((), jnp.bfloat16)
            zero = jnp.zeros((), jnp.bfloat16)
            q_low = jnp.where(lane < head_dim, q, jnp.where(lane == head_dim, one, zero))
            q_high = jnp.where(lane < head_dim, jnp.where(lane == 0, one, zero), q)
            scores = [lax.dot_general(q_aug, kbuf[m, side, 0:n_keys, :], (((1,), (1,)), ((), ())),
                                      preferred_element_type=jnp.float32)
                      for side, q_aug in ((0, q_low), (1, q_high))]
            gate = jnp.dot(h_rows, weight(pair_q, pair_q + pair_f), preferred_element_type=jnp.float32)
            up = jnp.dot(h_rows, weight(pair_q + pair_f, in_cols), preferred_element_type=jnp.float32)
            out = None
            for side in (0, 1):
                s = scores[side]
                diag = jnp.where(tri, s[:, n_keys - TILE:], MASKED)
                s = diag if i == 0 else jnp.concatenate([s[:, :n_keys - TILE], diag], axis=1)
                top = jnp.max(s, axis=1, keepdims=True)
                e = jnp.exp2((s - top) * exp_scale)
                p = (e * (1.0 / jnp.sum(e, axis=1, keepdims=True))).astype(jnp.bfloat16)
                o = jnp.dot(p, vbuf[m, side, 0:n_keys, :], preferred_element_type=jnp.float32)
                out = o if out is None else out + o
            joined[rows, 0:pair_q] = out.astype(jnp.bfloat16)
            gate = gate.astype(jnp.bfloat16).astype(jnp.float32)
            up = up.astype(jnp.bfloat16).astype(jnp.float32)
            half = 0.5 * gate
            joined[rows, pair_q:] = ((half + half * jnp.tanh(half)) * up).astype(jnp.bfloat16)
            w_out = wbig[n, :, :, :, :, in_cols:].reshape(d_model, pair_q + pair_f)
            acc[m, rows, :] += lax.dot_general(joined[rows, :], w_out, (((1,), (1,)), ((), ())),
                                               preferred_element_type=jnp.float32)

    def stage_z(m):
        def rows_of(r, carry):
            at = pl.multiple_of(r * 64, 64)
            other = pl.multiple_of((1 - core) * t_loc + at, 64)
            zsend[m, pl.ds(at, 64), :] = acc[m, pl.ds(other, 64), :].astype(jnp.bfloat16)
            return carry

        lax.fori_loop(0, t_loc // 64, rows_of, 0)
        send_z(m).start()

    def add_z(m):
        send_z(m).wait_recv()

        def rows_of(r, carry):
            at = pl.multiple_of(r * 64, 64)
            mine = pl.multiple_of(core * t_loc + at, 64)
            z_own = acc[m, pl.ds(mine, 64), :].astype(jnp.bfloat16).astype(jnp.float32)
            z_sum = z_own + zrecv[m, pl.ds(at, 64), :].astype(jnp.float32)
            xbuf[m, pl.ds(at, 64), :] = (xbuf[m, pl.ds(at, 64), :].astype(jnp.float32) + z_sum).astype(jnp.bfloat16)
            return carry

        lax.fori_loop(0, t_loc // 64, rows_of, 0)
        send_z(m).wait_send()

    for m in range(n_micro):
        load_x(m).start()
    small.step(0), step(0, 0), step(1, 0)
    small.step(1), step(0, 1), step(1, 1)
    small.step(2), step(0, 2)
    small.step(3), step(0, 3)
    small.step(4), step(0, 4)
    small.step(5), step(1, 2), step(2, 0)
    small.step(6), step(1, 3), step(2, 1)
    step(0, 5)

    for m in range(n_micro):
        load_x(m).wait()
    if DO_COMPUTE:
        for layer in range(n_layers):
            spread = wsmall[:, :, :, :, layer * 256 + 128:layer * 256 + 256].astype(jnp.float32).reshape(8, 128, 128)
            for k in range(8):
                gain_buf[layer, :, k * 128:(k + 1) * 128] = jnp.sum(spread[k], axis=0, keepdims=True)

    def layer_loop(layer, carry):
        if DO_COMPUTE:
            for m in range(n_micro):
                @pl.when(layer > 0)
                def _():
                    add_z(m)

                norm(m, layer)
                send_h(m).start()
            for m in range(n_micro):
                def clear(r, carry):
                    acc[m, pl.ds(pl.multiple_of(r * 64, 64), 64), :] = jnp.zeros((64, d_model), jnp.float32)
                    return carry

                lax.fori_loop(0, seq // 64, clear, 0)
                send_h(m).wait_recv()
                keys_values(m, layer)
            for m in range(n_micro):
                send_h(m).wait_send()

        def chunk_loop(it, carry):
            c, m = it // n_micro, lax.rem(it, n_micro)
            n = layer * n_chunks + c

            @pl.when(m == 0)
            def _():
                step(n, 6)
                step(n + 1, 4)
                step(n + 2, 2)
                step(n + 3, 0)

            @pl.when(m == 1)
            def _():
                step(n + 1, 5)
                step(n + 2, 3)
                step(n + 3, 1)

            if DO_COMPUTE:
                body(n, c, m)

                @pl.when(c == n_chunks - 1)
                def _():
                    stage_z(m)
            return carry

        lax.fori_loop(0, n_chunks * n_micro, chunk_loop, 0)
        return carry

    lax.fori_loop(0, n_layers, layer_loop, 0)
    for m in range(n_micro):
        if DO_COMPUTE:
            add_z(m)
        store_y(m).start()
    small.finish()

    def finish(n, carry):
        big(n).finish()
        return carry

    lax.fori_loop(0, n_total, finish, 0)
    for m in range(n_micro):
        store_y(m).wait()


def run_kernel(x_loc, lens, small, big, dims):
    n_micro, n_layers, n_chunks, t_loc, d_model, head_dim, ff_head = dims
    n_total = n_layers * n_chunks
    seq = 2 * t_loc
    any_spec = pl.BlockSpec(memory_space=pl.ANY)
    bf16 = jnp.bfloat16
    return pl.pallas_call(
        functools.partial(mesh_kernel, dims),
        out_shape=jax.ShapeDtypeStruct((n_micro, t_loc, d_model), bf16),
        in_specs=[any_spec, pl.BlockSpec(memory_space=pltpu.SMEM), any_spec, any_spec],
        out_specs=any_spec,
        scratch_shapes=[
            pltpu.VMEM((SIDE, SIDE, SIDE) + small.shape, bf16),
            pltpu.VMEM((n_total, SIDE, SIDE, SIDE) + big.shape[1:], bf16),
            pltpu.VMEM((n_micro, t_loc, d_model), bf16),
            pltpu.VMEM((n_micro, seq, d_model), bf16),
            pltpu.VMEM((n_micro, 2, seq, 2 * head_dim), bf16),
            pltpu.VMEM((n_micro, 2, seq, 2 * head_dim), bf16),
            pltpu.VMEM((n_micro, seq, d_model), jnp.float32),
            pltpu.VMEM((seq, 2 * (head_dim + ff_head)), bf16),
            pltpu.VMEM((n_micro, t_loc, d_model), bf16),
            pltpu.VMEM((n_micro, t_loc, d_model), bf16),
            pltpu.VMEM((n_layers, 1, d_model), jnp.float32),
            pltpu.SemaphoreType.DMA((n_total + 1,)),
            pltpu.SemaphoreType.DMA((n_total + 1, 6)),
            pltpu.SemaphoreType.DMA((n_total + 1, 6)),
            pltpu.SemaphoreType.DMA((n_micro,)),
            pltpu.SemaphoreType.DMA((n_micro,)),
            pltpu.SemaphoreType.DMA((n_micro,)),
            pltpu.SemaphoreType.DMA((n_micro,)),
            pltpu.SemaphoreType.DMA((n_micro,)),
        ],
        compiler_params=pltpu.CompilerParams(collective_id=0, has_side_effects=True, vmem_limit_bytes=67043328),
    )(x_loc, lens, small, big)


def pack(gain, w_in, w_kv, w_out, n_chunks):
    n_layers, rows, in_cols = w_in.shape
    head_dim = w_kv.shape[2] // 2
    out_rows = w_out.shape[1]
    heads = (out_rows * 2 - in_cols) // head_dim
    ff_head = out_rows // heads - head_dim
    w_in5 = w_in.reshape(n_layers, rows, n_chunks, 2, head_dim + 2 * ff_head)
    w_out5 = jnp.swapaxes(w_out, 1, 2).reshape(n_layers, rows, n_chunks, 2, head_dim + ff_head)
    lead = (n_layers, rows, n_chunks)
    big = jnp.concatenate([
        w_in5[..., :head_dim].reshape(lead + (-1,)),
        w_in5[..., head_dim:head_dim + ff_head].reshape(lead + (-1,)),
        w_in5[..., head_dim + ff_head:].reshape(lead + (-1,)),
        w_out5[..., :head_dim].reshape(lead + (-1,)),
        w_out5[..., head_dim:].reshape(lead + (-1,)),
    ], axis=-1)
    big = jnp.transpose(big, (0, 2, 1, 3)).reshape(n_layers * n_chunks, rows, -1)
    lane = rows * lax.rem(lax.axis_index("data"), 128 // rows)
    here = (lane + lax.broadcasted_iota(jnp.int32, (rows, 128), 0)) == lax.broadcasted_iota(jnp.int32, (rows, 128), 1)
    pieces = []
    for layer in range(n_layers):
        pieces.append(w_kv[layer])
        pieces.append(jnp.where(here, gain[layer][:, None], jnp.zeros((), gain.dtype)))
    return jnp.concatenate(pieces, axis=1), big, head_dim, ff_head


def solution(mesh):
    act_spec = P(None, ("part", "data"), "model", None)
    n_chunks = 4

    def local_fn(x_blk, len_blk, gain_blk, w_in_blk, w_kv_blk, w_out_blk):
        n_micro, _, t_loc, d_model = x_blk.shape
        small, big, head_dim, ff_head = pack(gain_blk, w_in_blk, w_kv_blk, w_out_blk, n_chunks)
        dims = (n_micro, gain_blk.shape[0], n_chunks, t_loc, d_model, head_dim, ff_head)
        y = run_kernel(x_blk.reshape(n_micro, t_loc, d_model), len_blk.reshape(n_micro), small, big, dims)
        return y.reshape(x_blk.shape)

    return jax.shard_map(
        local_fn,
        mesh=mesh,
        in_specs=(act_spec, P(None, ("part", "data")), P(None, "data"), P(None, "data", "model"), P(None, "data", None), P(None, "model", "data")),
        out_specs=act_spec,
        check_vma=False,
    )
```

time: 934 us -> 216 us (0.23); the launches traced: 922 us -> 216 us
  blocking collectives: 442 us -> 0 us
  matrix products: 213 us -> 0 us
  Pallas kernels: 0 us -> 204 us
  other arithmetic: 99.5 us -> 0.68 us
  starting transfers between devices: 60 us -> 0 us
  waiting for transfers between devices: 44.9 us -> 0 us
  local copies, waits for them, and re-layouts: 48.4 us -> 11.4 us
  between operations: 15 us -> 0.07 us
    all_gather x2 -> x0, blocking collectives: 288 us -> none  [local_fn(): w_kv_full = lax.all_gather(w_kv_blk[layer_idx], 'data', axis=0, tiled=True)]
    dot_general x20 -> x0, matrix products: 213 us -> none  [the longest x4 61.6 us: attention(): jnp.einsum('bhqk,bkc->bqhc', attn_probs, v_all, preferred_element_type=jn...]
    pallas_call x0 -> x1, Pallas kernels: none -> 204 us  [run_kernel(): pl.pallas_call(functools.partial(mesh_kernel, dims), out_shape=jax.ShapeD...]
    unnamed x1 -> x0, blocking collectives: 154 us -> none
    reduce_sum x12 -> x0, other arithmetic: 75.1 us -> none  [the longest x4 57.1 us: attention(): attn_probs = jax.nn.softmax(scores, axis=-1).astype(jnp.bfloat16)]
    all_to_all x4 -> x0, starting transfers between devices: 59.7 us -> none  [layer_block(): lax.all_to_all(group_sum.reshape(n_seqs, n_model, t_loc, d_model), 'model...]
    all_gather x8 -> x0, waiting for transfers between devices: 43 us -> none  [the longest x2 43 us: local_fn(): w_in_loc = lax.all_gather(w_in_blk[layer_idx], 'data', axis=0, tiled=True)]
    all_gather x4 -> x0, local copies, waits for them, and re-layouts: 41.6 us -> none  [the longest x2 25.4 us: local_fn(): w_in_loc = lax.all_gather(w_in_blk[layer_idx], 'data', axis=0, tiled=True)]
  transfers between devices with their start and end apart: 12 -> 0, of which waited for: 1 -> 0; matrix products, arithmetic and copies ran while one was open for 37% -> 0% of each run, Pallas kernels for 0% -> 0%
where the time goes in v1:
time: 216 us
  Pallas kernels  204 us (94%)
  local copies, waits for them, and re-layouts  11.4 us (5%)
    pallas_call x1, Pallas kernels, run_kernel(): pl.pallas_call(functools.partial(mesh_kernel, dims), out_shape=jax.ShapeD...  204 us
    unnamed x5, local copies, waits for them, and re-layouts  5.68 us

profile of v1, /device:TPU:1, one launch (start us, length us, event | category | flops | bytes accessed | tf_op | source)
XLA Modules:
  0.0 215.7 jit_solution(12493842211007623726)
XLA Ops:
  0.0 0.7 slice_bitcast_fusion.3
  0.7 0.1 fusion.1
  0.8 0.7 slice_bitcast_fusion.1
  1.5 0.6 pad_maximum_fusion.small_hbm
  2.1 1.1 reshape.41
  3.3 0.2 slice.40
  3.5 0.1 reshape.49
  3.6 0.1 reshape.50
  3.7 1.3 reshape.37
  5.1 0.4 fusion.2
  5.5 0.1 reshape.46
  5.6 0.1 reshape.48
  5.7 0.1 reshape.47
  5.8 0.6 copy_dynamic-update-slice_fusion.4
  6.4 0.7 copy_dynamic-update-slice_fusion.2
  7.1 0.7 copy_dynamic-update-slice_fusion.1
  7.8 0.6 copy_dynamic-update-slice_fusion.3
  8.4 0.7 copy_dynamic-update-slice_fusion
  9.1 203.5 %shard_map.64 = bf16[2,512,1024]{2,1,0:T(8,128)(2,1)} custom-call(bf16[2,512,1024]{2,1,0:T(8,128)(2,1)} %bitcast.18, s32[2]{0:T(128)} %bitcast.20, bf16[16,512]{1,0:T(8,128)(2,1)} %pad_maximum_fusion.small_hbm, bf16[8,16,1792]{2,1,0:T(8,128)(2,1)} %bitcast.8.big_hbm), custom_call_target="tpu_custom_call" | custom-call | tf_op jit(solution)/shard_map/pallas_call | solution.py:331
  212.6 3.1 %copy.28 = bf16[2,1,512,1024]{3,2,1,0:T(8,128)(2,1)} copy(bf16[2,1,512,1024]{3,2,1,0:T(8,128)(2,1)} %bitcast.17) | data formatting | bytes 4194304
  (3 shorter events, 0.1 us)

commit v2 on v1

v2 whole, which is shorter than its diff:
```python
import functools
import math

import jax
import jax.numpy as jnp
from jax import lax
from jax.experimental import pallas as pl
from jax.experimental.pallas import tpu as pltpu
from jax.sharding import PartitionSpec as P

MESH = pl.DeviceIdType.MESH
NORM_EPS = 1e-6
MASKED = -3e38
SIDE = 4
ROTATIONS = (("x", "y", "z"), ("y", "z", "x"), ("z", "x", "y"))
TILE = 256
BLOCK = 128
N_COMM = 99
DO_COMM = True
DO_COMPUTE = True


def mesh_kernel(dims, x_hbm, lens_ref, gain_ref, kv_ref, w_in_hbm, w_out_hbm, y_hbm,
                small, wsmall, wbig, xbuf, hbuf, kbuf, vbuf, acc, joined, zsend, zrecv, gain_buf,
                own_sem, wsend, wrecv, io_sem, hsend, hrecv, zs_sem, zr_sem):
    n_micro, n_layers, n_chunks, t_loc, d_model, head_dim, ff_head = dims
    n_total = n_layers * n_chunks
    pair_q, pair_f = 2 * head_dim, 2 * ff_head
    in_cols = pair_q + 2 * pair_f
    seq = 2 * t_loc
    me = lax.axis_index("data")
    core = lax.axis_index("model")
    pos = {"x": lax.rem(me, SIDE), "y": lax.rem(me // SIDE, SIDE), "z": me // (SIDE * SIDE)}
    stride = {"x": 1, "y": SIDE, "z": SIDE * SIDE}

    def shifted(axis, step):
        moved = lax.rem(pos[axis] + SIDE + step, SIDE)
        return moved, me + (moved - pos[axis]) * stride[axis]

    near = {(a, s): shifted(a, s) for a in "xyz" for s in (1, -1)}
    far = {a: shifted(a, 2) for a in "xyz"}
    sibling = {"model": 1 - core}

    barrier = pltpu.get_barrier_semaphore()
    for key in near:
        pl.semaphore_signal(barrier, inc=1, device_id={"data": near[key][1]}, device_id_type=MESH)
    for axis in "xyz":
        pl.semaphore_signal(barrier, inc=1, device_id={"data": far[axis][1]}, device_id_type=MESH)
    pl.semaphore_signal(barrier, inc=1, device_id=sibling, device_id_type=MESH)

    def load_x(m):
        return pltpu.make_async_copy(x_hbm.at[m], xbuf.at[m], io_sem.at[m])

    for m in range(n_micro):
        load_x(m).start()

    n_rows = kv_ref.shape[1]
    for layer in range(n_layers):
        small[:, layer * 128:(layer + 1) * 128] = kv_ref[layer]
    spread = (lax.rem(lax.broadcasted_iota(jnp.int32, (n_rows, 128), 1), n_rows)
              == lax.broadcasted_iota(jnp.int32, (n_rows, 128), 0)).astype(jnp.float32).astype(jnp.bfloat16)
    gains = jnp.dot(gain_ref[...], spread, preferred_element_type=jnp.float32)
    feature = lax.broadcasted_iota(jnp.int32, (n_rows, 128), 1) - n_rows * lax.rem(me, 128 // n_rows)
    row = lax.broadcasted_iota(jnp.int32, (n_rows, 128), 0)
    block = jnp.zeros((n_rows, 128), jnp.float32)
    for layer in range(n_layers):
        block = jnp.where(lax.rem(feature + layer, n_rows) == row, jnp.where(feature >= 0, jnp.where(
            feature < n_rows, gains[layer:layer + 1, :], block), block), block)
    small[:, n_layers * 128:] = block.astype(jnp.bfloat16)
    pl.semaphore_wait(barrier, 10)

    cut = 128 * ((in_cols // 128 + 1) // 2)
    out_cols = pair_q + pair_f
    big_parts = ((0, cut), (cut, in_cols), (in_cols, in_cols + out_cols))
    small_parts = ((0, 128), (128, 256), (256, 384))

    class Chunk:
        def __init__(self, buf, sources, parts, sem_idx, direct=()):
            self.buf, self.sources, self.parts, self.sem, self.direct = buf, sources, parts, sem_idx, direct

        def region(self, where, cols):
            return self.buf.at[where["z"], where["y"], where["x"], :, pl.ds(cols[0], cols[1] - cols[0])]

        def own(self):
            copies = []
            if self is first:
                return copies
            for j, (src, lo, hi) in enumerate(self.sources):
                dst = self.buf.at[pos["z"], pos["y"], pos["x"], :, pl.ds(lo, hi - lo)]
                copies.append(pltpu.make_async_copy(src, dst, own_sem.at[self.sem, j]))
            return copies

        def source(self, cols):
            for src, lo, hi in self.sources:
                if lo <= cols[0] and cols[1] <= hi:
                    return src.at[:, pl.ds(cols[0] - lo, cols[1] - cols[0])]

        def send(self, k):
            phase, second = k // 2, k % 2
            direct = phase in self.direct
            if direct and second:
                return
            for rot, (lo, hi) in zip(ROTATIONS, self.parts):
                axis = rot[phase]
                mid = lo + (((hi - lo) // 128 + 1) // 2) * 128
                for sign in (1, -1, 2)[:3 if direct else 2]:
                    where = {a: slice(None) for a in rot[:phase]}
                    where.update({a: pos[a] for a in rot[phase:]})
                    cols = (lo, hi)
                    if second:
                        where[axis] = near[axis, -sign][0]
                        if phase == 0:
                            cols = (lo, mid) if sign == 1 else (mid, hi)
                            if cols[0] == cols[1]:
                                continue
                        else:
                            where[rot[0]] = pl.ds(0, 2) if sign == 1 else pl.ds(2, 2)
                    dst = self.region(where, cols)
                    src = self.source(cols) if k == 0 else dst
                    pltpu.make_async_remote_copy(
                        src_ref=src, dst_ref=dst, send_sem=wsend.at[self.sem, k], recv_sem=wrecv.at[self.sem, k],
                        device_id={"data": far[axis][1] if sign == 2 else near[axis, sign][1]}, device_id_type=MESH).start()

        def bytes_of(self, k):
            count = 1 if k % 2 else 3 if k // 2 in self.direct else 2
            ref = (self.buf.at[0, 0, pl.ds(0, count)], self.buf.at[0, pl.ds(0, count)], self.buf.at[pl.ds(0, count)])[k // 2]
            return pltpu.make_async_remote_copy(
                src_ref=ref, dst_ref=ref, send_sem=wsend.at[self.sem, k], recv_sem=wrecv.at[self.sem, k],
                device_id={"data": near["x", 1][1]}, device_id_type=MESH)

        def step(self, k):
            if not DO_COMM:
                return
            if k == 0:
                for copy in self.own():
                    copy.start()
            elif k % 2 or k // 2 - 1 not in self.direct:
                self.bytes_of(k - 1).wait_recv()
            else:
                self.bytes_of(k - 2).wait_recv()
            if k == 2:
                for copy in self.own():
                    copy.wait()
            if k < 6:
                self.send(k)

        def finish(self):
            if not DO_COMM:
                return
            for k in range(6):
                if k % 2 == 0 or k // 2 not in self.direct:
                    self.bytes_of(k).wait_send()

    first = Chunk(wsmall, ((small, 0, 384),), small_parts, n_total, direct=(0, 1))

    def big(n):
        layer, c = n // n_chunks, n % n_chunks if isinstance(n, int) else lax.rem(n, n_chunks)

        def piece(ref, width):
            at = c * width if isinstance(c, int) else pl.multiple_of(c * width, 128)
            return ref.at[layer, :, pl.ds(at, width)]

        return Chunk(wbig.at[n], ((piece(w_in_hbm, in_cols), 0, in_cols),
                                  (piece(w_out_hbm, out_cols), in_cols, in_cols + out_cols)), big_parts, n,
                     direct=(0,) if isinstance(n, int) and n == 0 else ())

    def step(n, k):
        if isinstance(n, int):
            if n < min(n_total, N_COMM):
                big(n).step(k)
        else:
            @pl.when(n < min(n_total, N_COMM))
            def _():
                big(n).step(k)

    def store_y(m):
        return pltpu.make_async_copy(xbuf.at[m], y_hbm.at[m], io_sem.at[m])

    n_blocks = t_loc // BLOCK

    def send_h(m, r):
        rows = hbuf.at[m, pl.ds(pl.multiple_of(core * t_loc + r * BLOCK, BLOCK), BLOCK)]
        return pltpu.make_async_remote_copy(src_ref=rows, dst_ref=rows, send_sem=hsend.at[m, r], recv_sem=hrecv.at[m, r],
                                            device_id=sibling, device_id_type=MESH)

    def send_z(m, r):
        rows = pl.ds(pl.multiple_of(r * BLOCK, BLOCK), BLOCK)
        return pltpu.make_async_remote_copy(src_ref=zsend.at[m, rows], dst_ref=zrecv.at[m, rows], send_sem=zs_sem.at[m, r],
                                            recv_sem=zr_sem.at[m, r], device_id=sibling, device_id_type=MESH)

    def add_z(m, r):
        rows = pl.ds(pl.multiple_of(r * BLOCK, BLOCK), BLOCK)
        mine = pl.ds(pl.multiple_of(core * t_loc + r * BLOCK, BLOCK), BLOCK)
        send_z(m, r).wait_recv()
        z_own = acc[m, mine, :].astype(jnp.bfloat16).astype(jnp.float32)
        y = (xbuf[m, rows, :].astype(jnp.float32) + (z_own + zrecv[m, rows, :].astype(jnp.float32))).astype(jnp.bfloat16)
        xbuf[m, rows, :] = y
        acc[m, mine, :] = jnp.zeros((BLOCK, d_model), jnp.float32)
        send_z(m, r).wait_send()

    def norm(m, layer, after_z):
        def block_of(r, carry):
            if after_z:
                add_z(m, r)
            x_f32 = xbuf[m, pl.ds(pl.multiple_of(r * BLOCK, BLOCK), BLOCK), :].astype(jnp.float32)
            centered = x_f32 - jnp.mean(x_f32, axis=-1, keepdims=True)
            variance = jnp.mean(centered * centered, axis=-1, keepdims=True)
            h_act = (centered * lax.rsqrt(variance + NORM_EPS) * gain_buf[layer]).astype(jnp.bfloat16)
            hbuf[m, pl.ds(pl.multiple_of(core * t_loc + r * BLOCK, BLOCK), BLOCK), :] = h_act

            @pl.when(r > 0)
            def _():
                send_h(m, r - 1).start()
            return carry

        lax.fori_loop(0, n_blocks, block_of, 0)
        send_h(m, n_blocks - 1).start()

    def keys_values(m, layer):
        w_kv = wsmall[:, :, :, :, pl.ds(pl.multiple_of(layer * 128, 128), 128)].reshape(d_model, 2 * head_dim)
        lane = lax.broadcasted_iota(jnp.int32, (TILE, 2 * head_dim), 1)
        low = lane < head_dim
        length = lens_ref[m]

        def half(base):
            for t in range(t_loc // TILE):
                at = pl.multiple_of(base + t * TILE, TILE)
                rows = pl.ds(at, TILE)
                kv_f32 = jnp.dot(hbuf[m, rows, :], w_kv, preferred_element_type=jnp.float32)
                kv_f32 = kv_f32.astype(jnp.bfloat16).astype(jnp.float32)
                vk_f32 = pltpu.roll(kv_f32, head_dim, 1)
                key_pos = at + lax.broadcasted_iota(jnp.int32, (TILE, 2 * head_dim), 0)
                bias = jnp.where(key_pos < length, 0.0, MASKED)
                k_low = jnp.where(low, kv_f32, jnp.where(lane == head_dim, bias, 0.0))
                k_high = jnp.where(low, jnp.where(lane == 0, bias, 0.0), vk_f32)
                kbuf[m, 0, rows, :] = k_low.astype(jnp.bfloat16)
                kbuf[m, 1, rows, :] = k_high.astype(jnp.bfloat16)
                vbuf[m, 0, rows, :] = jnp.where(low, vk_f32, 0.0).astype(jnp.bfloat16)
                vbuf[m, 1, rows, :] = jnp.where(low, 0.0, kv_f32).astype(jnp.bfloat16)

        half(core * t_loc)
        for r in range(n_blocks):
            send_h(m, r).wait_recv()
        half((1 - core) * t_loc)
        for r in range(n_blocks):
            send_h(m, r).wait_send()

    exp_scale = (1.0 / math.sqrt(head_dim)) * math.log2(math.e)

    def body(n, m):
        lane = lax.broadcasted_iota(jnp.int32, (TILE, 2 * head_dim), 1)
        low = lane < head_dim
        seen = (lax.broadcasted_iota(jnp.int32, (TILE, TILE), 0) >= lax.broadcasted_iota(jnp.int32, (TILE, TILE), 1))
        w_in = wbig[n, :, :, :, :, :in_cols].reshape(d_model, in_cols)
        w_out = wbig[n, :, :, :, :, in_cols:].reshape(d_model, out_cols)
        one = jnp.ones((), jnp.bfloat16)
        zero = jnp.zeros((), jnp.bfloat16)
        unit = head_dim + 2 * ff_head
        n_tiles = seq // TILE
        proj, scores = {}, {}

        def rows(i):
            return slice(i * TILE, (i + 1) * TILE)

        def project(i):
            proj[i] = jnp.dot(hbuf[m, rows(i), :], w_in, preferred_element_type=jnp.float32).astype(jnp.bfloat16)

        def score(i):
            n_keys = (i + 1) * TILE
            at = unit - head_dim
            q_aug = (jnp.where(low, proj[i][:, :2 * head_dim], jnp.where(lane == head_dim, one, zero)),
                     jnp.where(low, jnp.where(lane == 0, one, zero), proj[i][:, at:at + 2 * head_dim]))
            for side in (0, 1):
                s = lax.dot_general(q_aug[side], kbuf[m, side, 0:n_keys, :], (((1,), (1,)), ((), ())),
                                    preferred_element_type=jnp.float32)
                diag = jnp.where(seen, s[:, n_keys - TILE:], MASKED)
                scores[i, side] = diag if i == 0 else jnp.concatenate([s[:, :n_keys - TILE], diag], axis=1)

        def softmax(s):
            top = jnp.max(s, axis=1, keepdims=True)
            e = jnp.exp2((s - top) * exp_scale)
            return (e * (1.0 / jnp.sum(e, axis=1, keepdims=True))).astype(jnp.bfloat16)

        def mlp(i, g_at, u_at, width):
            gate = proj[i][:, g_at:g_at + width].astype(jnp.float32)
            up = proj[i][:, u_at:u_at + width].astype(jnp.float32)
            half = 0.5 * gate
            return ((half + half * jnp.tanh(half)) * up).astype(jnp.bfloat16)

        def join(i):
            n_keys = (i + 1) * TILE
            probs = [softmax(scores.pop((i, side))) for side in (0, 1)]
            first = mlp(i, 0, ff_head, ff_head + 2 * head_dim)
            joined[rows(i), 2 * head_dim:ff_head] = first[:, 2 * head_dim:ff_head]
            joined[rows(i), ff_head + 2 * head_dim:] = mlp(i, unit + head_dim, unit + head_dim + ff_head, ff_head)
            outs = [jnp.dot(probs[side], vbuf[m, side, 0:n_keys, :], preferred_element_type=jnp.float32) for side in (0, 1)]
            pair = (outs[0] + outs[1]).astype(jnp.bfloat16)
            joined[rows(i), 0:2 * head_dim] = jnp.where(low, pair, first[:, :2 * head_dim])
            joined[rows(i), ff_head:ff_head + 2 * head_dim] = jnp.where(low, first[:, ff_head:], pair)

        def project_out(i):
            acc[m, rows(i), :] += lax.dot_general(joined[rows(i), :], w_out, (((1,), (1,)), ((), ())),
                                                  preferred_element_type=jnp.float32)

        order = list(range(n_tiles))[::-1]
        project(order[0])
        score(order[0])
        for at, i in enumerate(order):
            following = order[at + 1:at + 2]
            for j in following:
                project(j)
            join(i)
            for j in following:
                score(j)
            project_out(i)

    def stage_z(m):
        def block_of(r, carry):
            other = pl.ds(pl.multiple_of((1 - core) * t_loc + r * BLOCK, BLOCK), BLOCK)
            zsend[m, pl.ds(pl.multiple_of(r * BLOCK, BLOCK), BLOCK), :] = acc[m, other, :].astype(jnp.bfloat16)
            acc[m, other, :] = jnp.zeros((BLOCK, d_model), jnp.float32)

            @pl.when(r > 0)
            def _():
                send_z(m, r - 1).start()
            return carry

        lax.fori_loop(0, n_blocks, block_of, 0)
        send_z(m, n_blocks - 1).start()

    def boundary(layer, after_z):
        for m in range(n_micro):
            norm(m, layer, after_z)
        for m in range(n_micro):
            keys_values(m, layer)

    if DO_COMM:
        wsmall[pos["z"], pos["y"], pos["x"]] = small[...]
    first.step(0), step(0, 0), step(1, 0), step(2, 0)
    first.step(2), step(0, 2), step(1, 1), step(2, 1)
    first.step(4), step(0, 3), step(1, 2), step(2, 2)
    first.step(5), step(0, 4), step(1, 3), step(2, 3), step(3, 0), step(4, 0)
    if DO_COMPUTE:
        def clear(r, carry):
            for m in range(n_micro):
                acc[m, pl.ds(pl.multiple_of(r * 64, 64), 64), :] = jnp.zeros((64, d_model), jnp.float32)
            return carry

        lax.fori_loop(0, seq // 64, clear, 0)
    first.step(6)
    for m in range(n_micro):
        load_x(m).wait()
    if DO_COMPUTE:
        table = wsmall[:, :, :, :, n_layers * 128:].astype(jnp.float32).reshape(d_model // 128, 128, 128)
        lane = lax.broadcasted_iota(jnp.int32, (128, 128), 1)
        row = lax.broadcasted_iota(jnp.int32, (128, 128), 0)
        for layer in range(n_layers):
            mine = lax.rem(lane + layer, n_rows) == lax.rem(row, n_rows)
            for k in range(d_model // 128):
                gain_buf[layer, :, k * 128:(k + 1) * 128] = jnp.sum(jnp.where(mine, table[k], 0.0), axis=0, keepdims=True)
        norm(0, 0, False)
        norm(1, 0, False)
    step(0, 5), step(3, 1), step(4, 1), step(1, 4), step(3, 2), step(5, 0)
    if DO_COMPUTE:
        keys_values(0, 0)
        keys_values(1, 0)

    def layer_loop(layer, carry):
        if DO_COMPUTE:
            @pl.when(layer > 0)
            def _():
                boundary(layer, True)

        def chunk_loop(it, carry):
            c, m = it // n_micro, lax.rem(it, n_micro)
            n = layer * n_chunks + c

            @pl.when(m == 0)
            def _():
                step(n, 6)

            @pl.when(m == 1)
            def _():
                step(n + 1, 5)
                step(n + 2, 4)
                step(n + 3, 3)
                step(n + 4, 2)
                step(n + 5, 1)
                step(n + 6, 0)

            if DO_COMPUTE:
                body(n, m)

                @pl.when(c == n_chunks - 1)
                def _():
                    stage_z(m)
            return carry

        lax.fori_loop(0, n_chunks * n_micro, chunk_loop, 0)
        return carry

    lax.fori_loop(0, n_layers, layer_loop, 0)
    for m in range(n_micro):
        if DO_COMPUTE:
            for r in range(n_blocks):
                add_z(m, r)
        store_y(m).start()
    first.finish()
    step_zero = big(0)
    if N_COMM > 0:
        step_zero.finish()

    def finish(n, carry):
        big(n).finish()
        return carry

    lax.fori_loop(1, min(n_total, N_COMM), finish, 0)
    for m in range(n_micro):
        store_y(m).wait()


def run_kernel(x_loc, lens, gain, w_kv, w_in, w_out, dims):
    n_micro, n_layers, n_chunks, t_loc, d_model, head_dim, ff_head = dims
    n_total = n_layers * n_chunks
    seq = 2 * t_loc
    any_spec = pl.BlockSpec(memory_space=pl.ANY)
    vmem_spec = pl.BlockSpec(memory_space=pltpu.VMEM)
    bf16 = jnp.bfloat16
    rows = w_in.shape[1]
    small_cols = (n_layers + 1) * 128
    n_blocks = t_loc // BLOCK
    return pl.pallas_call(
        functools.partial(mesh_kernel, dims),
        out_shape=jax.ShapeDtypeStruct((n_micro, t_loc, d_model), bf16),
        in_specs=[any_spec, pl.BlockSpec(memory_space=pltpu.SMEM), vmem_spec, vmem_spec, any_spec, any_spec],
        out_specs=any_spec,
        scratch_shapes=[
            pltpu.VMEM((rows, small_cols), bf16),
            pltpu.VMEM((SIDE, SIDE, SIDE, rows, small_cols), bf16),
            pltpu.VMEM((n_total, SIDE, SIDE, SIDE, w_in.shape[1], (w_in.shape[2] + w_out.shape[2]) // n_chunks), bf16),
            pltpu.VMEM((n_micro, t_loc, d_model), bf16),
            pltpu.VMEM((n_micro, seq, d_model), bf16),
            pltpu.VMEM((n_micro, 2, seq, 2 * head_dim), bf16),
            pltpu.VMEM((n_micro, 2, seq, 2 * head_dim), bf16),
            pltpu.VMEM((n_micro, seq, d_model), jnp.float32),
            pltpu.VMEM((seq, 2 * (head_dim + ff_head)), bf16),
            pltpu.VMEM((n_micro, t_loc, d_model), bf16),
            pltpu.VMEM((n_micro, t_loc, d_model), bf16),
            pltpu.VMEM((n_layers, 1, d_model), jnp.float32),
            pltpu.SemaphoreType.DMA((n_total + 1, 2)),
            pltpu.SemaphoreType.DMA((n_total + 1, 6)),
            pltpu.SemaphoreType.DMA((n_total + 1, 6)),
            pltpu.SemaphoreType.DMA((n_micro,)),
            pltpu.SemaphoreType.DMA((n_micro, n_blocks)),
            pltpu.SemaphoreType.DMA((n_micro, n_blocks)),
            pltpu.SemaphoreType.DMA((n_micro, n_blocks)),
            pltpu.SemaphoreType.DMA((n_micro, n_blocks)),
        ],
        compiler_params=pltpu.CompilerParams(collective_id=0, has_side_effects=True, vmem_limit_bytes=67043328),
    )(x_loc, lens, gain, w_kv, w_in, w_out)


def solution(mesh):
    act_spec = P(None, ("part", "data"), "model", None)
    def local_fn(x_blk, len_blk, gain_blk, w_in_blk, w_kv_blk, w_out_blk):
        n_micro, _, t_loc, d_model = x_blk.shape
        head_dim = w_kv_blk.shape[2] // 2
        out_rows = w_out_blk.shape[1]
        heads = (2 * out_rows - w_in_blk.shape[2]) // head_dim
        ff_head = out_rows // heads - head_dim
        n_chunks = heads // 2
        dims = (n_micro, gain_blk.shape[0], n_chunks, t_loc, d_model, head_dim, ff_head)
        y = run_kernel(x_blk.reshape(n_micro, t_loc, d_model), len_blk.reshape(n_micro), gain_blk, w_kv_blk, w_in_blk,
                       jnp.swapaxes(w_out_blk, 1, 2), dims)
        return y.reshape(x_blk.shape)

    return jax.shard_map(
        local_fn,
        mesh=mesh,
        in_specs=(act_spec, P(None, ("part", "data")), P(None, "data"), P(None, "data", "model"), P(None, "data", None), P(None, "model", "data")),
        out_specs=act_spec,
        check_vma=False,
    )
```

time: 216 us -> 162 us (0.75)
  Pallas kernels: 204 us -> 159 us
  local copies, waits for them, and re-layouts: 11.4 us -> 3.08 us
    pallas_call x1, Pallas kernels: 204 us -> 159 us  [run_kernel(): pl.pallas_call(functools.partial(mesh_kernel, dims), out_shape=jax.ShapeD...]
    reshape x7 -> x0, local copies, waits for them, and re-layouts: 2.89 us -> none  [the longest x1 1.29 us: pack(): w_in5 = w_in.reshape(n_layers, rows, n_chunks, 2, head_dim + 2 * ff_head)]
    unnamed x5 -> x1, local copies, waits for them, and re-layouts: 5.68 us -> 3.08 us
where the time goes in v2:
time: 162 us
  Pallas kernels  159 us (98%)
  local copies, waits for them, and re-layouts  3.08 us (2%)
    pallas_call x1, Pallas kernels, run_kernel(): pl.pallas_call(functools.partial(mesh_kernel, dims), out_shape=jax.ShapeD...  159 us

profile of v2, /device:TPU:1, one launch (start us, length us, event | category | flops | bytes accessed | tf_op | source)
XLA Modules:
  0.0 161.7 jit_solution(2682300365205086996)
XLA Ops:
  0.0 158.6 %shard_map.64 = bf16[2,512,1024]{2,1,0:T(8,128)(2,1)} custom-call(bf16[2,512,1024]{2,1,0:T(8,128)(2,1)} %bitcast.7, s32[2]{0:T(128)} %bitcast.9, bf16[2,16]{1,0:T(2,128)(2,1)} %gain_ref.1, bf16[2,16,128]{2,1,0:T(8,128)(2,1)} %kv_ref.1, bf16[2,16,4608]{2,1,0:T(8,128)(2,1)} %w_in_hbm.1, bf16[2,16,2560]{2,1,0:T(8,128)(2,1)} %bitcast.8), custom_call_target="tpu_custom_call" | custom-call | tf_op jit(solution)/shard_map/pallas_call | solution.py:432
  158.6 3.1 %copy.9 = bf16[2,1,512,1024]{3,2,1,0:T(8,128)(2,1)} copy(bf16[2,1,512,1024]{3,2,1,0:T(8,128)(2,1)} %bitcast.6) | data formatting | bytes 4194304

commit v3 on v2

--- a/solution.py
+++ b/solution.py
@@ -16,8 +16,29 @@
 TILE = 256
 BLOCK = 128
 N_COMM = 99
+BODY = True
 DO_COMM = True
 DO_COMPUTE = True
+PLAN = (
+        (("f", 0), (0, 0), (1, 0), (2, 0), ("f", 2), (0, 2), (1, 1), (2, 1), ("f", 4), (0, 3), (1, 2), (2, 2), ("f", 5), (0,
+     4), (1, 3), (2, 3), (3, 0), (4, 0), ("CLEAR", 0), ("f", 6), ("GAIN", 0), ("N0", 0), ("N1", 0), (0, 5), (3, 1), (4, 1),
+     (1, 4), ("K0", 0), ("K1", 0), (0, 6), (3, 2), (5, 0)),
+        ((1, 5), (2, 4), (3, 3), (4, 2), (5, 1), (6, 0)),
+        ((1, 6),),
+        ((2, 5), (3, 4), (4, 3), (5, 2), (6, 1), (7, 0)),
+        ((2, 6),),
+        ((3, 5), (4, 4), (5, 3), (6, 2), (7, 1)),
+        ((3, 6),),
+        ((4, 5), (5, 4), (6, 3), (7, 2)),
+        (("N0", 0), ("N1", 0), ("K0", 0), ("K1", 0), (4, 6)),
+        ((5, 5), (6, 4), (7, 3)),
+        ((5, 6),),
+        ((6, 5), (7, 4)),
+        ((6, 6),),
+        ((7, 5),),
+        ((7, 6),),
+        (),
+)
 
 
 def mesh_kernel(dims, x_hbm, lens_ref, gain_ref, kv_ref, w_in_hbm, w_out_hbm, y_hbm,
@@ -75,7 +96,8 @@
     small_parts = ((0, 128), (128, 256), (256, 384))
 
     class Chunk:
-        def __init__(self, buf, sources, parts, sem_idx, direct=()):
+        def __init__(self, buf, sources, parts, sem_idx, direct=(), turn=0):
+            self.turn = turn
             self.buf, self.sources, self.parts, self.sem, self.direct = buf, sources, parts, sem_idx, direct
 
         def region(self, where, cols):
@@ -100,7 +122,8 @@
             direct = phase in self.direct
             if direct and second:
                 return
-            for rot, (lo, hi) in zip(ROTATIONS, self.parts):
+            for part, (lo, hi) in enumerate(self.parts):
+                rot = ROTATIONS[(part + self.turn) % 3]
                 axis = rot[phase]
                 mid = lo + (((hi - lo) // 128 + 1) // 2) * 128
                 for sign in (1, -1, 2)[:3 if direct else 2]:
@@ -162,16 +185,12 @@
 
         return Chunk(wbig.at[n], ((piece(w_in_hbm, in_cols), 0, in_cols),
                                   (piece(w_out_hbm, out_cols), in_cols, in_cols + out_cols)), big_parts, n,
-                     direct=(0,) if isinstance(n, int) and n == 0 else ())
+                     direct=(0,) if isinstance(n, int) and n == 0 else (),
+                     turn=n if isinstance(n, int) else 0)
 
     def step(n, k):
-        if isinstance(n, int):
-            if n < min(n_total, N_COMM):
-                big(n).step(k)
-        else:
-            @pl.when(n < min(n_total, N_COMM))
-            def _():
-                big(n).step(k)
+        if n < min(n_total, N_COMM):
+            big(n).step(k)
 
     def store_y(m):
         return pltpu.make_async_copy(xbuf.at[m], y_hbm.at[m], io_sem.at[m])
@@ -328,29 +347,15 @@
         lax.fori_loop(0, n_blocks, block_of, 0)
         send_z(m, n_blocks - 1).start()
 
-    def boundary(layer, after_z):
-        for m in range(n_micro):
-            norm(m, layer, after_z)
-        for m in range(n_micro):
-            keys_values(m, layer)
-
-    if DO_COMM:
-        wsmall[pos["z"], pos["y"], pos["x"]] = small[...]
-    first.step(0), step(0, 0), step(1, 0), step(2, 0)
-    first.step(2), step(0, 2), step(1, 1), step(2, 1)
-    first.step(4), step(0, 3), step(1, 2), step(2, 2)
-    first.step(5), step(0, 4), step(1, 3), step(2, 3), step(3, 0), step(4, 0)
-    if DO_COMPUTE:
-        def clear(r, carry):
+    def clear_acc():
+        def rows_of(r, carry):
             for m in range(n_micro):
                 acc[m, pl.ds(pl.multiple_of(r * 64, 64), 64), :] = jnp.zeros((64, d_model), jnp.float32)
             return carry
 
-        lax.fori_loop(0, seq // 64, clear, 0)
-    first.step(6)
-    for m in range(n_micro):
-        load_x(m).wait()
-    if DO_COMPUTE:
+        lax.fori_loop(0, seq // 64, rows_of, 0)
+
+    def read_gains():
         table = wsmall[:, :, :, :, n_layers * 128:].astype(jnp.float32).reshape(d_model // 128, 128, 128)
         lane = lax.broadcasted_iota(jnp.int32, (128, 128), 1)
         row = lax.broadcasted_iota(jnp.int32, (128, 128), 0)
@@ -358,48 +363,51 @@
             mine = lax.rem(lane + layer, n_rows) == lax.rem(row, n_rows)
             for k in range(d_model // 128):
                 gain_buf[layer, :, k * 128:(k + 1) * 128] = jnp.sum(jnp.where(mine, table[k], 0.0), axis=0, keepdims=True)
-        norm(0, 0, False)
-        norm(1, 0, False)
-    step(0, 5), step(3, 1), step(4, 1), step(1, 4), step(3, 2), step(5, 0)
-    if DO_COMPUTE:
-        keys_values(0, 0)
-        keys_values(1, 0)
-
-    def layer_loop(layer, carry):
+
+    def run(event, layer):
+        name, k = event
+        if name == "f":
+            first.step(k)
+        elif not isinstance(name, str):
+            step(name, k)
+        elif DO_COMPUTE and name == "CLEAR":
+            clear_acc()
+        elif DO_COMPUTE and name == "GAIN":
+            read_gains()
+        elif name in ("N0", "N1"):
+            m = int(name[1])
+            if layer == 0:
+                load_x(m).wait()
+            if DO_COMPUTE:
+                norm(m, layer, layer > 0)
+        elif DO_COMPUTE:
+            keys_values(int(name[1]), layer)
+
+    if DO_COMM:
+        wsmall[pos["z"], pos["y"], pos["x"]] = small[...]
+    per_layer = n_chunks * n_micro
+    for event in PLAN[0]:
+        run(event, 0)
+
+    def body_loop(it, carry):
+        for at in range(1, len(PLAN)):
+            if PLAN[at]:
+                @pl.when(it == at)
+                def _(at=at):
+                    for event in PLAN[at]:
+                        run(event, at // per_layer)
+
         if DO_COMPUTE:
-            @pl.when(layer > 0)
+            n, m = it // n_micro, lax.rem(it, n_micro)
+            if BODY:
+                body(n, m)
+
+            @pl.when(lax.rem(it, per_layer) >= per_layer - n_micro)
             def _():
-                boundary(layer, True)
-
-        def chunk_loop(it, carry):
-            c, m = it // n_micro, lax.rem(it, n_micro)
-            n = layer * n_chunks + c
-
-            @pl.when(m == 0)
-            def _():
-                step(n, 6)
-
-            @pl.when(m == 1)
-            def _():
-                step(n + 1, 5)
-                step(n + 2, 4)
-                step(n + 3, 3)
-                step(n + 4, 2)
-                step(n + 5, 1)
-                step(n + 6, 0)
-
-            if DO_COMPUTE:
-                body(n, m)
-
-                @pl.when(c == n_chunks - 1)
-                def _():
-                    stage_z(m)
-            return carry
-
-        lax.fori_loop(0, n_chunks * n_micro, chunk_loop, 0)
+                stage_z(m)
         return carry
 
-    lax.fori_loop(0, n_layers, layer_loop, 0)
+    lax.fori_loop(0, len(PLAN), body_loop, 0)
     for m in range(n_micro):
         if DO_COMPUTE:
             for r in range(n_blocks):

time: 162 us -> 162 us (level)
  no operation moved by 1% of the time
where the time goes in v3:
time: 162 us; the launch traced here: 161 us
  Pallas kernels  158 us (98%)
  local copies, waits for them, and re-layouts  3.08 us (2%)
    pallas_call x1, Pallas kernels, run_kernel(): pl.pallas_call(functools.partial(mesh_kernel, dims), out_shape=jax.ShapeD...  158 us

profile of v3, /device:TPU:1, one launch (start us, length us, event | category | flops | bytes accessed | tf_op | source)
XLA Modules:
  0.0 161.4 jit_solution(17282572170844426178)
XLA Ops:
  0.0 158.3 %shard_map.64 = bf16[2,512,1024]{2,1,0:T(8,128)(2,1)} custom-call(bf16[2,512,1024]{2,1,0:T(8,128)(2,1)} %bitcast.7, s32[2]{0:T(128)} %bitcast.9, bf16[2,16]{1,0:T(2,128)(2,1)} %gain_ref.1, bf16[2,16,128]{2,1,0:T(8,128)(2,1)} %kv_ref.1, bf16[2,16,4608]{2,1,0:T(8,128)(2,1)} %w_in_hbm.1, bf16[2,16,2560]{2,1,0:T(8,128)(2,1)} %bitcast.8), custom_call_target="tpu_custom_call" | custom-call | tf_op jit(solution)/shard_map/pallas_call | solution.py:440
  158.3 3.1 %copy.9 = bf16[2,1,512,1024]{3,2,1,0:T(8,128)(2,1)} copy(bf16[2,1,512,1024]{3,2,1,0:T(8,128)(2,1)} %bitcast.6) | data formatting | bytes 4194304
